TPU v7x, 256 devices: a whole 4x4x8 slice. The times are simulated.
256 devices in a mesh: pts: 32 (over x, y, core), med: 8 (over z).
Axes of the slice: x: 4, y: 4, z: 8, core: 2. Of those that a mesh axis runs over, the one named last changes fastest.
Arguments:
- sketches: bfloat16 [32768, 4096], P('pts'), may hold values from -12 to 12
- assignment: int32 [32768], P('pts'), may hold values from 0 to 4095
- medoid_ids: int32 [4096], P('med'), may hold values from 0 to 32767, as said below
Outputs:
- gap: float32 [32768], P('pts')
- coverage: float32 [], replicated
- weights: float32 [4096], P('med')
- gradient_sums: float32 [4096, 4096], P('pts', 'med')
Inputs may be any that keep to these rules, and one draw needn't show every extreme that they name: `medoid_ids`: the 4096 medoid ids are distinct point indices.
All inputs are finite; a program needn't handle non-finite values.
Results may differ from a plain program's by a relative error of at most 0.0003.
Values may be sent and summed in bfloat16 or wider, within the bound.
No kernel may reach another device: no remote copies, remote signals or barrier semaphores. Data moves between devices by JAX's collectives and lax.ppermute only.
A program may use at most 64 MiB of HBM per device.

v0:
```python
import jax
import jax.numpy as jnp
from jax import lax
from jax.sharding import PartitionSpec as P


def from_everyone(array, axis):
    size = lax.axis_size(axis)
    return lax.all_to_all(
        jnp.broadcast_to(array[None], (size, *array.shape)), axis, 0, 0, tiled=True
    )


def over_copies(array, axis):
    return from_everyone(array, axis).sum(axis=0)


def together(arrays, axis):
    line, at, done = (jnp.concatenate([a.reshape(-1) for a in arrays]), 0, [])
    running = over_copies(line, axis)
    for a in arrays:
        done.append(running[at : at + a.size].reshape(a.shape))
        at += a.size
    return tuple(done)


def shards(sketches, assignment, medoid_ids):
    row_count, feat_width = sketches.shape
    medoid_count = medoid_ids.shape[0]
    pts_count = lax.axis_size("pts")
    pts_index = lax.axis_index("pts")
    med_index = lax.axis_index("med")
    medoid_iota = jnp.arange(medoid_count, dtype=jnp.int32)
    local_assign = assignment - med_index * medoid_count
    one_hot = (local_assign[:, None] == medoid_iota[None, :]).astype(jnp.bfloat16)
    offsets = medoid_ids - pts_index * row_count
    inside = (offsets >= 0) & (offsets < row_count)
    picked = jnp.take(sketches, jnp.clip(offsets, 0, row_count - 1), axis=0)
    fetch_terms = jnp.where(inside[:, None], picked, jnp.zeros_like(picked))
    medoid_slice = (
        lax.psum_scatter(fetch_terms, "pts", scatter_dimension=1, tiled=True)
        .astype(jnp.float32)
        .astype(jnp.bfloat16)
    )
    gradient_sums = lax.psum_scatter(
        lax.dot_general(
            sketches, one_hot, (((0,), (0,)), ((), ())), preferred_element_type=jnp.float32
        ),
        "pts",
        scatter_dimension=0,
        tiled=True,
    )
    count_terms = jnp.sum(one_hot.astype(jnp.float32), axis=0)
    raw_scores = lax.dot_general(
        sketches,
        lax.all_gather(medoid_slice, "pts", axis=1, tiled=True),
        (((1,), (1,)), ((), ())),
        preferred_element_type=jnp.float32,
    )
    scores = raw_scores * (1.0 / feat_width)
    best_local = jnp.max(scores, axis=1)
    in_shard = (local_assign >= 0) & (local_assign < medoid_count)
    taken = jnp.take_along_axis(
        scores, jnp.clip(local_assign, 0, medoid_count - 1)[:, None], axis=1
    )[:, 0]
    assigned_local = jnp.where(in_shard, taken, -1e30)
    best_score, assigned = lax.pmax((best_local, assigned_local), "med")
    gap = best_score - assigned
    weights, cover_total = together((count_terms, jnp.sum(best_score)), "pts")
    coverage = cover_total / (row_count * pts_count)
    return (gap, coverage, weights, gradient_sums)


def solution(mesh):
    in_specs = (P("pts", None), P("pts"), P("med"))
    out_specs = (P("pts"), P(), P("med"), P("pts", "med"))
    return jax.shard_map(shards, mesh=mesh, in_specs=in_specs, out_specs=out_specs, check_vma=False)
```

profile of v0, /device:TPU:2, one launch (start us, length us, event | category | flops | bytes accessed | tf_op | source)
XLA Modules:
  0.0 295.6 jit_solution(7401411365770368771)
XLA Ops:
  7.2 0.0 reduce-scatter.7.cloned.1.call-start
  7.2 0.7 compare_and_fusion
  7.9 13.1 %gather_fusion = bf16[512,4096]{1,0:T(8,128)(2,1)} fusion(bf16[1024,4096]{1,0:T(8,128)(2,1)} %param.3, s32[1024]{0:T(1024)S(1)} %pad_clamp_fusion), kind=kCustom, calls=%fused_computation | custom fusion | bytes 8390656 | tf_op jit(solution)/shard_map/jit(_take)/gather | solution.py:38
  21.0 4.0 %select_select_fusion = bf16[512,4096]{1,0:T(8,128)(2,1)} fusion(bf16[512,4096]{1,0:T(8,128)(2,1)} %gather_fusion, pred[512]{0:T(512)(128)(4,1)S(1)} %get-tuple-element.28, pred[512]{0:T(512)(128)(4,1)S(1)} %get-tuple-element.34), kind=kLoop, calls=%fused_computation.3 | loop fusion | flops 4194304 | bytes 8389632 | tf_op jit(solution)/shard_map/jit(_where)/select_n | solution.py:39
  25.0 6.5 %copy.13 = bf16[512,4096]{0,1:T(8,128)(2,1)} copy(bf16[512,4096]{1,0:T(8,128)(2,1)} %select_select_fusion) | data formatting | bytes 8388608
  31.5 0.0 all-gather.2.cloned.1.call-start
  31.5 92.7 %reduce-scatter.7.cloned.1.call-done = bf16[128,512]{1,0:T(8,128)(2,1)} async-done(((bf16[4096,512]{1,0:T(8,128)(2,1)}), bf16[128,512]{1,0:T(8,128)(2,1)}) %reduce-scatter.7.cloned.1.call-update) | async-done | bytes 131088
  124.2 1.7 copy.14
  125.9 0.0 reduce-scatter.5.cloned.1.call-start
  126.0 10.4 %convolution_bitcast_fusion = f32[4096,512]{0,1:T(8,128)} fusion(bf16[1024,4096]{1,0:T(8,128)(2,1)} %param.3, s32[1024]{0:T(1024)S(1)} %get-tuple-element.27), kind=kOutput, calls=%fused_computation.2 | convolution fusion | flops 4295491584 | bytes 16781312 | tf_op jit(solution)/shard_map/dot_general | solution.py:46
  136.4 0.3 convert_reduce_fusion
  136.7 43.6 %all-gather.2.cloned.1.call-done = bf16[512,4096]{1,0:T(8,128)(2,1)} async-done(((bf16[512,128]{1,0:T(8,128)(2,1)}), bf16[512,4096]{1,0:T(8,128)(2,1)}) %all-gather.2.cloned.1.call-update) | async-done | bytes 4194320 | tf_op jit(solution)/shard_map/all_gather | solution.py:56
  180.3 8.3 %multiply_bitcast_fusion = (f32[1024,512]{0,1:T(8,128)S(1)}, f32[1024]{0:T(1024)S(1)}) fusion(bf16[512,4096]{1,0:T(8,128)(2,1)} %all-gather.2.cloned.1.call-done, bf16[1024,4096]{1,0:T(8,128)(2,1)} %param.3), kind=kOutput, calls=%fused_computation.7 | convolution fusion | flops 4296014848 | bytes 14684160 | tf_op jit(solution)/shard_map/dot_general | solution.py:54
  188.6 8.6 %gather_fusion.1 = f32[1024]{0:T(1024)S(1)} fusion(f32[1024,512]{0,1:T(8,128)S(1)} %get-tuple-element.30, s32[1024]{0:T(1024)S(1)} %bitcast.15), kind=kCustom, calls=%fused_computation.1 | custom fusion | bytes 16384 | tf_op jit(solution)/shard_map/jit(take_along_axis)/gather | solution.py:63
  197.2 17.7 %all-reduce = (f32[1024]{0:T(1024)S(1)}, f32[1024]{0:T(1024)S(1)}) all-reduce(f32[1024]{0:T(1024)S(1)} %get-tuple-element.31, f32[1024]{0:T(1024)S(1)} %select_select_fusion.1), channel_id=1, replica_groups=mesh['pts'=32,'med'=8] {'med'}, use_global_device_ids=true, to_apply=%region_2.3 | all-reduce | flops 2048 | bytes 16384 | tf_op jit(solution)/shard_map/pmax | solution.py:67
  215.0 1.2 fusion.5
  216.2 0.7 pad_maximum_fusion
  216.8 0.7 broadcast_in_dim.48
  217.5 6.0 %all-to-all-start = ((f32[32,1,513]{2,1,0:T(1,128)}), f32[32,1,513]{2,1,0:T(1,128)S(1)}, u32[]{:S(2)}, u32[]{:S(2)}) async-start(f32[32,1,513]{2,1,0:T(1,128)} %broadcast_in_dim.48), calls=%async_computation | async-start | bytes 163840 | tf_op jit(solution)/shard_map/all_to_all | solution.py:9
  223.5 60.8 %reduce-scatter.5.cloned.1.call-done = f32[128,512]{0,1:T(8,128)} async-done(((f32[4096,512]{0,1:T(8,128)}), f32[128,512]{0,1:T(8,128)}) %reduce-scatter.5.cloned.1.call-update) | async-done | bytes 262160 | tf_op jit(solution)/shard_map/reduce_scatter | solution.py:45
  284.3 1.8 copy.12
  286.1 0.1 reduce_sum.29
  286.2 0.5 slice.6
  286.7 0.6 slice.7
  (12 shorter events, 0.1 us)
Async XLA Ops:
  7.2 117.1 %reduce-scatter.7.cloned.1.call-start = ((), (), s32[]{:S(2)}) async-start(), calls=%async_computation.5 | async-start | bytes 4325376
  31.4 94.5 %copy-start = (s32[1024]{0:T(1024)S(1)}, s32[1024]{0:T(1024)}, u32[]{:S(2)}) copy-start(s32[1024]{0:T(1024)} %param.4) | copy-start | bytes 12292
  31.5 148.8 %all-gather.2.cloned.1.call-start = ((), (), s32[]{:S(2)}) async-start(), calls=%async_computation.3 | async-start | bytes 4325376 | tf_op jit(solution)/shard_map/all_gather | solution.py:56
  125.9 158.4 %reduce-scatter.5.cloned.1.call-start = ((), (), s32[]{:S(2)}) async-start(), calls=%async_computation.4 | async-start | bytes 8650752 | tf_op jit(solution)/shard_map/reduce_scatter | solution.py:45
  217.5 68.6 %all-to-all-start = ((f32[32,1,513]{2,1,0:T(1,128)}), f32[32,1,513]{2,1,0:T(1,128)S(1)}, u32[]{:S(2)}, u32[]{:S(2)}) async-start(f32[32,1,513]{2,1,0:T(1,128)} %broadcast_in_dim.48), calls=%async_computation | async-start | bytes 163840 | tf_op jit(solution)/shard_map/all_to_all | solution.py:9
Sparse Core Ops, SparseCore 0:
  31.6 92.5 reduce-scatter.6
  127.3 52.9 all-gather.1
  184.3 99.9 reduce-scatter.4
where the time goes:
time: 296 us
  waiting for transfers between devices  197 us (67%)
  local copies, waits for them, and re-layouts  33.4 us (11%)
  matrix products  18.6 us (6%)
  blocking collectives  17.7 us (6%)
  between operations  15.6 us (5%)
  other arithmetic  6.93 us (2%)
  starting transfers between devices  6.15 us (2%)
    unnamed x4, waiting for transfers between devices  92.8 us
    reduce_scatter x1, waiting for transfers between devices, shards(): lax.psum_scatter(lax.dot_general(sketches, one_hot, (((0,), (0,)), ((), (...  60.8 us
    all_gather x1, waiting for transfers between devices, shards(): lax.all_gather(medoid_slice, 'pts', axis=1, tiled=True)  43.6 us
    pmax x1, blocking collectives, shards(): best_score, assigned = lax.pmax((best_local, assigned_local), 'med')  17.7 us
    gather x1, local copies, waits for them, and re-layouts, shards(): picked = jnp.take(sketches, jnp.clip(offsets, 0, row_count - 1), axis=0)  13.1 us
    dot_general x1, matrix products, shards(): lax.dot_general(sketches, one_hot, (((0,), (0,)), ((), ())), preferred_el...  10.4 us
    unnamed x6, local copies, waits for them, and re-layouts  9.92 us
    gather x1, local copies, waits for them, and re-layouts, shards(): jnp.take_along_axis(scores, jnp.clip(local_assign, 0, medoid_count - 1)[:...  8.65 us
  transfers between devices with their start and end apart: 4, of which 3 were waited for; matrix products, arithmetic and copies ran while one was open for 11% of the time, Pallas kernels for 0%

commit v1 on v0

--- a/solution.py
+++ b/solution.py
@@ -2,6 +2,11 @@
 import jax.numpy as jnp
 from jax import lax
 from jax.sharding import PartitionSpec as P
+
+
+def gather_by_exchange(shard, axis, dim):
+    copies = jnp.concatenate([shard] * lax.axis_size(axis), axis=dim)
+    return lax.all_to_all(copies, axis, dim, dim, tiled=True)
 
 
 def from_everyone(array, axis):
@@ -53,7 +58,7 @@
     count_terms = jnp.sum(one_hot.astype(jnp.float32), axis=0)
     raw_scores = lax.dot_general(
         sketches,
-        lax.all_gather(medoid_slice, "pts", axis=1, tiled=True),
+        gather_by_exchange(medoid_slice, "pts", 1),
         (((1,), (1,)), ((), ())),
         preferred_element_type=jnp.float32,
     )

time: 296 us -> 262 us (0.89)
  waiting for transfers between devices: 197 us -> 133 us
  blocking collectives: 17.7 us -> 35.3 us
  local copies, waits for them, and re-layouts: 33.4 us -> 43.6 us
    reduce_scatter x1, waiting for transfers between devices: 60.8 us -> 0.02 us  [shards(): lax.psum_scatter(lax.dot_general(sketches, one_hot, (((0,), (0,)), ((), (...]
    all_to_all x1, waiting for transfers between devices: 0.01 us -> 50.8 us  [gather_by_exchange(): return lax.all_to_all(copies, axis, dim, dim, tiled=True)]
    all_gather x1 -> x0, waiting for transfers between devices: 43.6 us -> none  [shards(): lax.all_gather(medoid_slice, 'pts', axis=1, tiled=True)]
    all_to_all x0 -> x1, blocking collectives: none -> 17.6 us  [from_everyone(): lax.all_to_all(jnp.broadcast_to(array[None], (size, *array.shape)), axis,...]
    unnamed x4 -> x3, waiting for transfers between devices: 92.8 us -> 81.7 us
    all_to_all x0 -> x2, local copies, waits for them, and re-layouts: none -> 9.62 us  [gather_by_exchange(): return lax.all_to_all(copies, axis, dim, dim, tiled=True)]
    unnamed x6 -> x37, local copies, waits for them, and re-layouts: 9.92 us -> 11.1 us
  transfers between devices with their start and end apart: 4 -> 3, of which waited for: 3 -> 2; matrix products, arithmetic and copies ran while one was open for 11% -> 16% of each run, Pallas kernels for 0% -> 0%
where the time goes in v1:
time: 262 us; the launch traced here: 259 us
  waiting for transfers between devices  133 us (51%)
  local copies, waits for them, and re-layouts  43.6 us (17%)
  blocking collectives  35.3 us (13%)
  matrix products  18.8 us (7%)
  between operations  16.2 us (6%)
  other arithmetic  6.88 us (3%)
  starting transfers between devices  5.98 us (2%)
    unnamed x3, waiting for transfers between devices  81.7 us
    all_to_all x1, waiting for transfers between devices, gather_by_exchange(): return lax.all_to_all(copies, axis, dim, dim, tiled=True)  50.8 us
    pmax x1, blocking collectives, shards(): best_score, assigned = lax.pmax((best_local, assigned_local), 'med')  17.7 us
    all_to_all x1, blocking collectives, from_everyone(): lax.all_to_all(jnp.broadcast_to(array[None], (size, *array.shape)), axis,...  17.6 us
    gather x1, local copies, waits for them, and re-layouts, shards(): picked = jnp.take(sketches, jnp.clip(offsets, 0, row_count - 1), axis=0)  13 us
    unnamed x37, local copies, waits for them, and re-layouts  11.1 us
    dot_general x1, matrix products, shards(): lax.dot_general(sketches, one_hot, (((0,), (0,)), ((), ())), preferred_el...  10.4 us
    all_to_all x2, local copies, waits for them, and re-layouts, gather_by_exchange(): return lax.all_to_all(copies, axis, dim, dim, tiled=True)  9.62 us
  transfers between devices with their start and end apart: 3, of which 2 were waited for; matrix products, arithmetic and copies ran while one was open for 16% of the time, Pallas kernels for 0%

profile of v1, /device:TPU:2, one launch (start us, length us, event | category | flops | bytes accessed | tf_op | source)
XLA Modules:
  0.0 259.3 jit_solution(9608430654124263275)
XLA Ops:
  7.2 0.7 compare_and_fusion
  7.9 13.0 %gather_fusion = bf16[512,4096]{1,0:T(8,128)(2,1)} fusion(bf16[1024,4096]{1,0:T(8,128)(2,1)} %param.3, s32[1024]{0:T(1024)S(1)} %pad_clamp_fusion), kind=kCustom, calls=%fused_computation | custom fusion | bytes 8390656 | tf_op jit(solution)/shard_map/jit(_take)/gather | solution.py:43
  20.9 3.9 %select_select_fusion = bf16[512,4096]{1,0:T(8,128)(2,1)} fusion(bf16[512,4096]{1,0:T(8,128)(2,1)} %gather_fusion, pred[512]{0:T(512)(128)(4,1)S(1)} %get-tuple-element.32, pred[512]{0:T(512)(128)(4,1)S(1)} %get-tuple-element.38), kind=kLoop, calls=%fused_computation.4 | loop fusion | flops 4194304 | bytes 8389632 | tf_op jit(solution)/shard_map/jit(_where)/select_n | solution.py:44
  24.9 6.5 %copy.21 = bf16[512,4096]{0,1:T(8,128)(2,1)} copy(bf16[512,4096]{1,0:T(8,128)(2,1)} %select_select_fusion) | data formatting | bytes 8388608
  31.4 0.0 reduce-scatter.5.cloned.1.call-start
  31.5 0.6 copy-done
  32.1 10.4 %convolution_bitcast_fusion = f32[4096,512]{0,1:T(8,128)} fusion(bf16[1024,4096]{1,0:T(8,128)(2,1)} %param.3, s32[1024]{0:T(1024)S(1)} %get-tuple-element.31), kind=kOutput, calls=%fused_computation.2 | convolution fusion | flops 4295491584 | bytes 16781312 | tf_op jit(solution)/shard_map/dot_general | solution.py:51
  42.5 81.7 %reduce-scatter.7.cloned.1.call-done = bf16[128,512]{1,0:T(8,128)(2,1)} async-done(((bf16[4096,512]{1,0:T(8,128)(2,1)}), bf16[128,512]{1,0:T(8,128)(2,1)}) %reduce-scatter.7.cloned.1.call-update) | async-done | bytes 131088
  124.2 1.0 copy.22
  126.7 3.1 %copy_bitcast_fusion = bf16[512,32,128]{2,0,1:T(8,128)(2,1)} fusion(bf16[512,4096]{1,0:T(8,128)(2,1)S(1)} %constant_dynamic-update-slice_fusion), kind=kLoop, calls=%fused_computation.3 | loop fusion | bytes 8388608 | tf_op jit(solution)/shard_map/all_to_all | solution.py:9
  129.8 5.9 %all-to-all-start = ((bf16[512,32,128]{2,0,1:T(8,128)(2,1)}), bf16[512,32,128]{2,0,1:T(8,128)(2,1)}, u32[]{:S(2)}, u32[]{:S(2)}) async-start(bf16[512,32,128]{2,0,1:T(8,128)(2,1)} %copy_bitcast_fusion), calls=%async_computation | async-start | bytes 8388608 | tf_op jit(solution)/shard_map/all_to_all | solution.py:9
  135.8 0.3 convert_reduce_fusion
  136.1 50.8 %all-to-all-done = bf16[512,32,128]{2,0,1:T(8,128)(2,1)} async-done(((bf16[512,32,128]{2,0,1:T(8,128)(2,1)}), bf16[512,32,128]{2,0,1:T(8,128)(2,1)}, u32[]{:S(2)}, u32[]{:S(2)}) %all-to-all-start) | async-done | bytes 4194336 | tf_op jit(solution)/shard_map/all_to_all | solution.py:9
  186.9 6.5 %copy.18 = bf16[512,32,128]{0,2,1:T(8,128)(2,1)} copy(bf16[512,32,128]{2,0,1:T(8,128)(2,1)} %all-to-all-done) | data formatting | bytes 8388608 | tf_op jit(solution)/shard_map/all_to_all | solution.py:9
  193.4 8.5 %multiply_bitcast_fusion = (f32[1024,512]{0,1:T(8,128)S(1)}, f32[1024]{0:T(1024)S(1)}) fusion(bf16[512,4096]{0,1:T(8,128)(2,1)} %bitcast.23, bf16[1024,4096]{1,0:T(8,128)(2,1)} %param.3), kind=kOutput, calls=%fused_computation.8 | convolution fusion | flops 4296014848 | bytes 14684160 | tf_op jit(solution)/shard_map/dot_general | solution.py:59
  201.8 8.6 %gather_fusion.1 = f32[1024]{0:T(1024)S(1)} fusion(f32[1024,512]{0,1:T(8,128)S(1)} %get-tuple-element.34, s32[1024]{0:T(1024)S(1)} %bitcast.21), kind=kCustom, calls=%fused_computation.1 | custom fusion | bytes 16384 | tf_op jit(solution)/shard_map/jit(take_along_axis)/gather | solution.py:68
  210.5 17.7 %all-reduce = (f32[1024]{0:T(1024)S(1)}, f32[1024]{0:T(1024)S(1)}) all-reduce(f32[1024]{0:T(1024)S(1)} %get-tuple-element.35, f32[1024]{0:T(1024)S(1)} %select_select_fusion.1), channel_id=1, replica_groups=mesh['pts'=32,'med'=8] {'med'}, use_global_device_ids=true, to_apply=%region_2.3 | all-reduce | flops 2048 | bytes 16384 | tf_op jit(solution)/shard_map/pmax | solution.py:72
  228.2 1.2 fusion.5
  229.4 0.7 pad_maximum_fusion
  230.1 17.6 %all_to_all.18 = f32[32,1,513]{2,1,0:T(1,128)S(1)} all-to-all(f32[32,1,513]{2,1,0:T(1,128)S(1)} %broadcast_in_dim.48), channel_id=1, replica_groups=mesh['pts'=32,'med'=8] {'pts'}, dimensions={0} | all-to-all | bytes 131328 | tf_op jit(solution)/shard_map/all_to_all | solution.py:14
  247.7 0.1 reduce_sum.29
  247.8 0.5 slice.6
  248.3 0.6 slice.7
  249.5 1.8 copy.20
  (44 shorter events, 1.4 us)
Async XLA Ops:
  7.2 117.0 %reduce-scatter.7.cloned.1.call-start = ((), (), s32[]{:S(2)}) async-start(), calls=%async_computation.5 | async-start | bytes 4325376
  31.4 0.7 copy-start
  31.4 218.1 %reduce-scatter.5.cloned.1.call-start = ((), (), s32[]{:S(2)}) async-start(), calls=%async_computation.4 | async-start | bytes 8650752 | tf_op jit(solution)/shard_map/reduce_scatter | solution.py:50
  129.8 57.0 %all-to-all-start = ((bf16[512,32,128]{2,0,1:T(8,128)(2,1)}), bf16[512,32,128]{2,0,1:T(8,128)(2,1)}, u32[]{:S(2)}, u32[]{:S(2)}) async-start(bf16[512,32,128]{2,0,1:T(8,128)(2,1)} %copy_bitcast_fusion), calls=%async_computation | async-start | bytes 8388608 | tf_op jit(solution)/shard_map/all_to_all | solution.py:9
Sparse Core Ops, SparseCore 0:
  31.5 92.5 reduce-scatter.6
  128.2 101.9 reduce-scatter.4
